TPU v7x, 32 devices: a 4x4x1 block of a 4x4x8 slice. The times are simulated.
32 devices in a mesh: dp: 1 (over z), sp: 32 (over y, x, core).
Axes of the slice: x: 4, y: 4, z: 1, core: 2. Of those that a mesh axis runs over, the one named last changes fastest.
The devices are a block of a 4x4x8 slice.
Arguments:
- signal: bfloat16 [65536, 2560], P(('dp', 'sp'))
- w_first: bfloat16 [10, 1024, 2, 64, 64], P(None, 'sp')
- w_second: bfloat16 [10, 1024, 2, 64, 64], P(None, 'sp')
Outputs:
- output: bfloat16 [65536, 2560], P(('dp', 'sp'))
All inputs are finite; a program needn't handle non-finite values.
Results may differ from a plain program's by a relative error of at most 0.02.
Values are sent between devices in bfloat16 or wider.
A program may use at most 768 MiB of HBM per device.

v0:
```python
import jax
import jax.numpy as jnp
from jax import lax
from jax.sharding import PartitionSpec as P


def local_partner(act_blocks, distance):
    num_blocks = act_blocks.shape[0]
    grouped = act_blocks.reshape(num_blocks // (2 * distance), 2, distance, act_blocks.shape[1], act_blocks.shape[2])
    return grouped[:, ::-1].reshape(act_blocks.shape)


def mix_blocks(act_blocks, partner, weights):
    own_part = jnp.einsum("lij,ljc->lic", weights[:, 0], act_blocks, preferred_element_type=jnp.float32)
    cross_part = jnp.einsum("lij,ljc->lic", weights[:, 1], partner, preferred_element_type=jnp.float32)
    return (own_part + cross_part).astype(jnp.bfloat16)


def solution(mesh):
    groups = mesh.shape["sp"]

    def apply_map(act_blocks, weights, distances):
        local_blocks = act_blocks.shape[0]
        for stage, distance in enumerate(distances):
            if distance < local_blocks:
                partner = local_partner(act_blocks, distance)
            else:
                dev_step = distance // local_blocks
                pairing = [(device, device ^ dev_step) for device in range(groups)]
                partner = lax.ppermute(act_blocks, "sp", pairing)
            act_blocks = mix_blocks(act_blocks, partner, weights[stage])
        return act_blocks

    def device_program(signal, w_first, w_second):
        stages = w_first.shape[0]
        local_blocks = w_first.shape[1]
        block_rows = w_first.shape[3]
        act_blocks = signal.reshape(local_blocks, block_rows, signal.shape[1])
        dist_down = [2 ** (stages - 1 - level) for level in range(stages)]
        hidden = apply_map(act_blocks, w_first, dist_down)
        hidden = jax.nn.gelu(hidden.astype(jnp.float32), approximate=False).astype(jnp.bfloat16)
        result = apply_map(hidden, w_second, dist_down[::-1])
        return result.reshape(signal.shape)

    row_spec = P(("dp", "sp"), None)
    weight_spec = P(None, "sp", None, None, None)
    return jax.shard_map(device_program, mesh=mesh, in_specs=(row_spec, weight_spec, weight_spec), out_specs=row_spec, check_vma=False)
```

profile of v0, /device:TPU:97, one launch (start us, length us, event | category | flops | bytes accessed | tf_op | source)
XLA Modules:
  0.0 2433.5 jit_solution(5542834124638912072)
XLA Ops:
  20.9 209.3 %collective-permute-done = bf16[32,64,2560]{2,1,0:T(8,128)(2,1)} collective-permute-done((bf16[32,64,2560]{2,1,0:T(8,128)(2,1)}, bf16[32,64,2560]{2,1,0:T(8,128)(2,1)}, u32[]{:S(2)}, u32[]{:S(2)}) %collective-permute-start) | collective-permute-done | bytes 10485792 | tf_op jit(solution)/shard_map/ppermute | solution.py:30
  262.0 209.8 %collective-permute-done.1 = bf16[32,64,2560]{2,1,0:T(8,128)(2,1)} collective-permute-done((bf16[32,64,2560]{2,1,0:T(8,128)(2,1)}, bf16[32,64,2560]{2,1,0:T(8,128)(2,1)}, u32[]{:S(2)}, u32[]{:S(2)}) %collective-permute-start.1) | collective-permute-done | bytes 10485792 | tf_op jit(solution)/shard_map/ppermute | solution.py:30
  471.7 15.8 add_convert_fusion.18
  505.7 208.5 %collective-permute-done.2 = bf16[32,64,2560]{2,1,0:T(8,128)(2,1)} collective-permute-done((bf16[32,64,2560]{2,1,0:T(8,128)(2,1)}, bf16[32,64,2560]{2,1,0:T(8,128)(2,1)}, u32[]{:S(2)}, u32[]{:S(2)}) %collective-permute-start.2) | collective-permute-done | bytes 10485792 | tf_op jit(solution)/shard_map/ppermute | solution.py:30
  714.2 16.0 add_convert_fusion.17
  745.3 209.0 %collective-permute-done.3 = bf16[32,64,2560]{2,1,0:T(8,128)(2,1)} collective-permute-done((bf16[32,64,2560]{2,1,0:T(8,128)(2,1)}, bf16[32,64,2560]{2,1,0:T(8,128)(2,1)}, u32[]{:S(2)}, u32[]{:S(2)}) %collective-permute-start.3) | collective-permute-done | bytes 10485792 | tf_op jit(solution)/shard_map/ppermute | solution.py:30
  997.7 16.2 add_convert_fusion.15
  1036.7 15.8 add_convert_fusion.14
  1075.4 16.0 add_convert_fusion.13
  1114.3 15.8 add_convert_fusion.12
  1153.0 16.0 add_convert_fusion.11
  1191.9 49.5 %fusion.2 = bf16[32,64,2560]{2,1,0:T(8,128)(2,1)S(1)} fusion(f32[32,2560,64]{1,2,0:T(8,128)} %fusion.42, bf16[32,64,2560]{2,1,0:T(8,128)(2,1)} %bitcast.394, bf16[32,2,64,64]{3,2,0,1:T(8,128)(2,1)S(1)} %copy-done.17), kind=kOutput, calls=%fused_computation.5 | convolution fusion | flops 1027604480 | bytes 42467328 | tf_op jit(solution)/shard_map/lij,ljc->lic/dot_general | solution.py:15
  1260.8 16.2 add_convert_fusion.9
  1299.9 15.8 add_convert_fusion.8
  1338.6 16.0 add_convert_fusion.7
  1377.5 15.9 add_convert_fusion.6
  1416.2 16.0 add_convert_fusion.5
  1479.4 211.7 %collective-permute-done.6 = bf16[32,64,2560]{2,1,0:T(8,128)(2,1)} collective-permute-done((bf16[32,64,2560]{2,1,0:T(8,128)(2,1)}, bf16[32,64,2560]{2,1,0:T(8,128)(2,1)}, u32[]{:S(2)}, u32[]{:S(2)}) %collective-permute-start.6) | collective-permute-done | bytes 10485792 | tf_op jit(solution)/shard_map/ppermute | solution.py:30
  1723.7 210.8 %collective-permute-done.7 = bf16[32,64,2560]{2,1,0:T(8,128)(2,1)} collective-permute-done((bf16[32,64,2560]{2,1,0:T(8,128)(2,1)}, bf16[32,64,2560]{2,1,0:T(8,128)(2,1)}, u32[]{:S(2)}, u32[]{:S(2)}) %collective-permute-start.7) | collective-permute-done | bytes 10485792 | tf_op jit(solution)/shard_map/ppermute | solution.py:30
  1934.5 16.0 add_convert_fusion.2
  1964.9 210.7 %collective-permute-done.8 = bf16[32,64,2560]{2,1,0:T(8,128)(2,1)} collective-permute-done((bf16[32,64,2560]{2,1,0:T(8,128)(2,1)}, bf16[32,64,2560]{2,1,0:T(8,128)(2,1)}, u32[]{:S(2)}, u32[]{:S(2)}) %collective-permute-start.8) | collective-permute-done | bytes 10485792 | tf_op jit(solution)/shard_map/ppermute | solution.py:30
  2175.6 15.8 add_convert_fusion.1
  2207.7 209.6 %collective-permute-done.9 = bf16[32,64,2560]{2,1,0:T(8,128)(2,1)} collective-permute-done((bf16[32,64,2560]{2,1,0:T(8,128)(2,1)}, bf16[32,64,2560]{2,1,0:T(8,128)(2,1)}, u32[]{:S(2)}, u32[]{:S(2)}) %collective-permute-start.9) | collective-permute-done | bytes 10485792 | tf_op jit(solution)/shard_map/ppermute | solution.py:30
  2417.3 15.8 add_convert_fusion
  (114 shorter events, 464.6 us)
Async XLA Ops:
  0.0 230.2 %collective-permute-start = (bf16[32,64,2560]{2,1,0:T(8,128)(2,1)}, bf16[32,64,2560]{2,1,0:T(8,128)(2,1)}, u32[]{:S(2)}, u32[]{:S(2)}) collective-permute-start(bf16[32,64,2560]{2,1,0:T(8,128)(2,1)} %bitcast.390), channel_id=1, source_target_pairs={{0,16},{1,17},{2,18},{3,19},{4,20},{5,21},{6,22},{7,23},{8,24},{9,... | collective-permute-start | bytes 31457288 | tf_op jit(solution)/shard_map/ppermute | solution.py:30
  246.0 225.7 %collective-permute-start.1 = (bf16[32,64,2560]{2,1,0:T(8,128)(2,1)}, bf16[32,64,2560]{2,1,0:T(8,128)(2,1)}, u32[]{:S(2)}, u32[]{:S(2)}) collective-permute-start(bf16[32,64,2560]{2,1,0:T(8,128)(2,1)} %add_convert_fusion.19), channel_id=1, source_target_pairs={{0,8},{1,9},{2,10},{3,11},{4,12},{5,13},{6,14},{7,15},{8,0},{9,1},... | collective-permute-start | bytes 31457288 | tf_op jit(solution)/shard_map/ppermute | solution.py:30
  487.5 226.7 %collective-permute-start.2 = (bf16[32,64,2560]{2,1,0:T(8,128)(2,1)}, bf16[32,64,2560]{2,1,0:T(8,128)(2,1)}, u32[]{:S(2)}, u32[]{:S(2)}) collective-permute-start(bf16[32,64,2560]{2,1,0:T(8,128)(2,1)} %bitcast.375), channel_id=1, source_target_pairs={{0,4},{1,5},{2,6},{3,7},{4,0},{5,1},{6,2},{7,3},{8,12},{9,13},{10,... | collective-permute-start | bytes 31457288 | tf_op jit(solution)/shard_map/ppermute | solution.py:30
  730.2 224.1 %collective-permute-start.3 = (bf16[32,64,2560]{2,1,0:T(8,128)(2,1)}, bf16[32,64,2560]{2,1,0:T(8,128)(2,1)}, u32[]{:S(2)}, u32[]{:S(2)}) collective-permute-start(bf16[32,64,2560]{2,1,0:T(8,128)(2,1)} %bitcast.376), channel_id=1, source_target_pairs={{0,2},{1,3},{2,0},{3,1},{4,6},{5,7},{6,4},{7,5},{8,10},{9,11},{10,... | collective-permute-start | bytes 31457288 | tf_op jit(solution)/shard_map/ppermute | solution.py:30
  970.1 14.9 copy-start.13
  970.1 27.6 %collective-permute-start.4 = (bf16[32,64,2560]{2,1,0:T(8,128)(2,1)}, bf16[32,64,2560]{2,1,0:T(8,128)(2,1)}, u32[]{:S(2)}, u32[]{:S(2)}) collective-permute-start(bf16[32,64,2560]{2,1,0:T(8,128)(2,1)} %bitcast.371), channel_id=1, source_target_pairs={{0,1},{1,0},{2,3},{3,2},{4,5},{5,4},{6,7},{7,6},{8,9},{9,8},{10,11... | collective-permute-start | bytes 31457288 | tf_op jit(solution)/shard_map/ppermute | solution.py:30
  1036.7 15.9 copy-start.7
  1075.4 16.0 copy-start.6
  1153.0 16.1 copy-start.17
  1191.9 49.5 %copy-start.5 = (bf16[32,2,64,64]{3,2,0,1:T(8,128)(2,1)S(1)}, bf16[32,2,64,64]{3,2,0,1:T(8,128)(2,1)}, u32[]{:S(2)}) copy-start(bf16[32,2,64,64]{3,2,0,1:T(8,128)(2,1)} %get-tuple-element.29) | copy-start | bytes 1572868
  1260.8 16.2 copy-start.4
  1299.9 15.9 copy-start.3
  1338.6 16.0 copy-start.2
  1377.5 15.9 copy-start.1
  1416.2 16.3 copy-start.12
  1432.3 16.2 collective-permute-start.5
  1446.5 19.0 copy-start.11
  1464.2 226.9 %collective-permute-start.6 = (bf16[32,64,2560]{2,1,0:T(8,128)(2,1)}, bf16[32,64,2560]{2,1,0:T(8,128)(2,1)}, u32[]{:S(2)}, u32[]{:S(2)}) collective-permute-start(bf16[32,64,2560]{2,1,0:T(8,128)(2,1)} %bitcast.378), channel_id=1, source_target_pairs={{0,2},{1,3},{2,0},{3,1},{4,6},{5,7},{6,4},{7,5},{8,10},{9,11},{10,... | collective-permute-start | bytes 31457288 | tf_op jit(solution)/shard_map/ppermute | solution.py:30
  1479.4 230.4 %copy-start.10 = (bf16[1,32,2,64,64]{4,3,2,1,0:T(8,128)(2,1)S(1)}, bf16[1,32,2,64,64]{4,3,2,1,0:T(8,128)(2,1)}, u32[]{:S(2)}) copy-start(bf16[1,32,2,64,64]{4,3,2,1,0:T(8,128)(2,1)} %get-tuple-element.12) | copy-start | bytes 1572868
  1706.9 227.6 %collective-permute-start.7 = (bf16[32,64,2560]{2,1,0:T(8,128)(2,1)}, bf16[32,64,2560]{2,1,0:T(8,128)(2,1)}, u32[]{:S(2)}, u32[]{:S(2)}) collective-permute-start(bf16[32,64,2560]{2,1,0:T(8,128)(2,1)} %bitcast.379), channel_id=1, source_target_pairs={{0,4},{1,5},{2,6},{3,7},{4,0},{5,1},{6,2},{7,3},{8,12},{9,13},{10,... | collective-permute-start | bytes 31457288 | tf_op jit(solution)/shard_map/ppermute | solution.py:30
  1723.7 227.3 %copy-start.9 = (bf16[1,32,2,64,64]{4,3,2,1,0:T(8,128)(2,1)S(1)}, bf16[1,32,2,64,64]{4,3,2,1,0:T(8,128)(2,1)}, u32[]{:S(2)}) copy-start(bf16[1,32,2,64,64]{4,3,2,1,0:T(8,128)(2,1)} %get-tuple-element.13) | copy-start | bytes 1572868
  1950.5 225.1 %collective-permute-start.8 = (bf16[32,64,2560]{2,1,0:T(8,128)(2,1)}, bf16[32,64,2560]{2,1,0:T(8,128)(2,1)}, u32[]{:S(2)}, u32[]{:S(2)}) collective-permute-start(bf16[32,64,2560]{2,1,0:T(8,128)(2,1)} %bitcast.380), channel_id=1, source_target_pairs={{0,8},{1,9},{2,10},{3,11},{4,12},{5,13},{6,14},{7,15},{8,0},{9,1},... | collective-permute-start | bytes 31457288 | tf_op jit(solution)/shard_map/ppermute | solution.py:30
  1964.9 228.8 %copy-start.8 = (bf16[1,32,2,64,64]{4,3,2,1,0:T(8,128)(2,1)S(1)}, bf16[1,32,2,64,64]{4,3,2,1,0:T(8,128)(2,1)}, u32[]{:S(2)}) copy-start(bf16[1,32,2,64,64]{4,3,2,1,0:T(8,128)(2,1)} %get-tuple-element.5) | copy-start | bytes 1572868
  2191.4 225.9 %collective-permute-start.9 = (bf16[32,64,2560]{2,1,0:T(8,128)(2,1)}, bf16[32,64,2560]{2,1,0:T(8,128)(2,1)}, u32[]{:S(2)}, u32[]{:S(2)}) collective-permute-start(bf16[32,64,2560]{2,1,0:T(8,128)(2,1)} %bitcast.374), channel_id=1, source_target_pairs={{0,16},{1,17},{2,18},{3,19},{4,20},{5,21},{6,22},{7,23},{8,24},{9,... | collective-permute-start | bytes 31457288 | tf_op jit(solution)/shard_map/ppermute | solution.py:30
  (10 other events, 122.4 us)
where the time goes:
time: 2450 us; the launch traced here: 2430 us
  waiting for transfers between devices  1680 us (69%)
  matrix products  613 us (25%)
  local copies, waits for them, and re-layouts  117 us (5%)
    ppermute x10, waiting for transfers between devices, apply_map(): partner = lax.ppermute(act_blocks, 'sp', pairing)  1680 us
    dot_general x20, matrix products, mix_blocks(): jnp.einsum('lij,ljc->lic', weights[:, 1], partner, preferred_element_type...  352 us
    dot_general x20, matrix products, mix_blocks(): jnp.einsum('lij,ljc->lic', weights[:, 0], act_blocks, preferred_element_t...  261 us
    rev x10, local copies, waits for them, and re-layouts, local_partner(): return grouped[:, ::-1].reshape(act_blocks.shape)  90.1 us
  transfers between devices with their start and end apart: 10, of which 9 were waited for; matrix products, arithmetic and copies ran while one was open for 6% of the time, Pallas kernels for 0%

commit v1 on v0

v1 whole, which is shorter than its diff:
```python
import functools

import jax
import jax.numpy as jnp
from jax import lax
from jax.experimental import pallas as pl
from jax.experimental.pallas import tpu as pltpu
from jax.sharding import PartitionSpec as P

MESH = pl.DeviceIdType.MESH
CHUNKS = 5
UNROLL = 4


def gelu(x):
    return 0.5 * x * (1.0 + lax.erf(x * (0.5 ** 0.5)))


def stage(src, dst, weights, s, dist, activate=False):
    blocks, rows, _ = src.shape

    def pairs(group, carry):
        for member in range(UNROLL):
            pair = group * UNROLL + member
            low = (pair // dist) * (2 * dist) + pair % dist
            high = low + dist
            mat = jnp.concatenate([weights[s, low], weights[s, high]], axis=0)
            act = jnp.concatenate([src[low], src[high]], axis=0)
            mixed = jnp.dot(mat, act, preferred_element_type=jnp.float32).astype(jnp.bfloat16)
            if activate:
                mixed = gelu(mixed.astype(jnp.float32)).astype(jnp.bfloat16)
            dst[low] = mixed[:rows]
            dst[high] = mixed[rows:]
        return carry

    lax.fori_loop(0, blocks // 2 // UNROLL, pairs, 0)


def kernel(n, signal, rows_first, rows_second, out, buf1, buf2, buf3, ping, pong,
           far_first, far_second, near_first, near_second, send_sems, recv_sems, wsend_sems, wrecv_sems, near_sems):
    me = lax.axis_index("sp")
    far = far_first.shape[0]
    chunks, blocks, block_rows, width = buf1.shape

    near1 = pltpu.make_async_copy(rows_first.at[pl.ds(far, far)], near_first, near_sems.at[0])
    near2 = pltpu.make_async_copy(rows_second.at[pl.ds(0, far)], near_second, near_sems.at[1])
    near1.start()
    near2.start()

    barrier = pltpu.get_barrier_semaphore()

    def greet(k, carry):
        pl.semaphore_signal(barrier, inc=1, device_id={"sp": lax.rem(me + k, n)}, device_id_type=MESH)
        return carry

    lax.fori_loop(1, n, greet, 0)
    pl.semaphore_wait(barrier, n - 1)

    def spread(src_of, dst, send_sem, recv_sem):
        def one(k, carry):
            peer = lax.rem(me + k, n)
            pltpu.make_async_remote_copy(
                src_ref=src_of(peer), dst_ref=dst, send_sem=send_sem, recv_sem=recv_sem,
                device_id={"sp": peer}, device_id_type=MESH).start()
            return carry

        lax.fori_loop(1, n, one, 0)

    def wait_bytes(ref, sem):
        pltpu.make_async_copy(ref, ref, sem).wait()

    def rows_of(block):
        return pl.ds(pl.multiple_of(block * block_rows, block_rows), block_rows)

    def columns_of(chunk):
        return pl.ds(pl.multiple_of(chunk * width, width), width)

    def send_signal(chunk, carry):
        cols = columns_of(chunk)
        spread(lambda peer: signal.at[rows_of(peer), cols], buf1.at[chunk, me], send_sems.at[0, chunk], recv_sems.at[0, chunk])
        pltpu.make_async_copy(signal.at[rows_of(me), cols], buf1.at[chunk, me], recv_sems.at[0, chunk]).start()
        return carry

    def send_weights(rows, base, dst, slot):
        spread(lambda peer: rows.at[pl.ds(base, far), peer], dst.at[:, me], wsend_sems.at[slot], wrecv_sems.at[slot])
        pltpu.make_async_copy(rows.at[pl.ds(base, far), me], dst.at[:, me], wrecv_sems.at[slot]).start()

    send_signal(0, 0)
    send_weights(rows_first, 0, far_first, 0)
    lax.fori_loop(1, chunks, send_signal, 0)
    send_weights(rows_second, far, far_second, 1)

    def exchange(chunk, src, dst, phase):
        spread(lambda peer: src.at[chunk, peer], dst.at[chunk, me], send_sems.at[phase, chunk], recv_sems.at[phase, chunk])
        dst[chunk, me] = src[chunk, me]

    wait_bytes(far_first, wrecv_sems.at[0])

    def first_far(chunk, carry):
        wait_bytes(buf1.at[chunk], recv_sems.at[0, chunk])
        refs = [buf1.at[chunk]] + [(ping, pong)[s % 2] for s in range(far - 1)] + [buf1.at[chunk]]
        for s in range(far):
            stage(refs[s], refs[s + 1], far_first, s, 2 ** (far - 1 - s))
        exchange(chunk, buf1, buf2, 1)
        return carry

    lax.fori_loop(0, chunks, first_far, 0)
    near1.wait()
    near2.wait()

    def middle(chunk, carry):
        wait_bytes(buf2.at[chunk, pl.ds(0, n - 1)], recv_sems.at[1, chunk])
        refs = [buf2.at[chunk]] + [(ping, pong)[s % 2] for s in range(2 * far - 1)] + [buf2.at[chunk]]
        for s in range(far):
            stage(refs[s], refs[s + 1], near_first, s, 2 ** (far - 1 - s), activate=s == far - 1)
        for s in range(far):
            stage(refs[far + s], refs[far + s + 1], near_second, s, 2 ** s)
        exchange(chunk, buf2, buf3, 2)
        return carry

    lax.fori_loop(0, chunks, middle, 0)
    wait_bytes(far_second, wrecv_sems.at[1])

    def second_far(chunk, carry):
        wait_bytes(buf3.at[chunk, pl.ds(0, n - 1)], recv_sems.at[2, chunk])
        refs = [buf3.at[chunk]] + [(ping, pong)[s % 2] for s in range(far - 1)] + [buf3.at[chunk]]
        for s in range(far):
            stage(refs[s], refs[s + 1], far_second, s, 2 ** s)
        dst = out.at[rows_of(me), columns_of(chunk)]
        spread(lambda peer: buf3.at[chunk, peer], dst, send_sems.at[3, chunk], recv_sems.at[3, chunk])
        pltpu.make_async_copy(buf3.at[chunk, me], dst, recv_sems.at[3, chunk]).start()
        return carry

    lax.fori_loop(0, chunks, second_far, 0)

    def finish(chunk, carry):
        wait_bytes(out.at[:, columns_of(chunk)], recv_sems.at[3, chunk])
        for phase in range(4):
            wait_bytes(buf1.at[chunk, pl.ds(0, n - 1)], send_sems.at[phase, chunk])
        return carry

    lax.fori_loop(0, chunks, finish, 0)
    for slot in range(2):
        wait_bytes(far_first.at[:, pl.ds(0, n - 1)], wsend_sems.at[slot])


def solution(mesh):
    n = mesh.shape["sp"]

    def weight_rows(weights, distances):
        stages, blocks, two, size, _ = weights.shape
        block = lax.axis_index("sp") * blocks + jnp.arange(blocks)
        upper = (block[None, :] // jnp.array(distances)[:, None]) % 2 == 1
        own_first = jnp.concatenate([weights[:, :, 0], weights[:, :, 1]], axis=-1)
        own_last = jnp.concatenate([weights[:, :, 1], weights[:, :, 0]], axis=-1)
        return jnp.where(upper[:, :, None, None], own_last, own_first)

    def device_program(signal, w_first, w_second):
        stages, blocks, _, block_rows, _ = w_first.shape
        far = stages // 2
        width = signal.shape[1] // CHUNKS
        dist_down = [2 ** (stages - 1 - level) for level in range(stages)]
        rows_first = weight_rows(w_first, dist_down)
        rows_second = weight_rows(w_second, dist_down[::-1])
        buf = pltpu.VMEM((CHUNKS, blocks, block_rows, width), jnp.bfloat16)
        half = pltpu.VMEM((blocks, block_rows, width), jnp.bfloat16)
        mats = pltpu.VMEM((far, blocks, block_rows, 2 * block_rows), jnp.bfloat16)
        return pl.pallas_call(
            functools.partial(kernel, n),
            out_shape=jax.ShapeDtypeStruct(signal.shape, signal.dtype),
            in_specs=[pl.BlockSpec(memory_space=pl.ANY)] * 3,
            out_specs=pl.BlockSpec(memory_space=pl.ANY),
            scratch_shapes=[buf, buf, buf, half, half, mats, mats, mats, mats,
                            pltpu.SemaphoreType.DMA((4, CHUNKS)), pltpu.SemaphoreType.DMA((4, CHUNKS)),
                            pltpu.SemaphoreType.DMA((2,)), pltpu.SemaphoreType.DMA((2,)), pltpu.SemaphoreType.DMA((2,))],
            compiler_params=pltpu.CompilerParams(collective_id=0, has_side_effects=True, vmem_limit_bytes=62 * 1024 * 1024),
        )(signal, rows_first, rows_second)

    row_spec = P(("dp", "sp"), None)
    weight_spec = P(None, "sp", None, None, None)
    return jax.shard_map(device_program, mesh=mesh, in_specs=(row_spec, weight_spec, weight_spec), out_specs=row_spec, check_vma=False)
```

time: 2450 us -> 632 us (0.26)
  waiting for transfers between devices: 1680 us -> 0 us
  matrix products: 613 us -> 0 us
  Pallas kernels: 0 us -> 576 us
  local copies, waits for them, and re-layouts: 117 us -> 32.2 us
    ppermute x10 -> x0, waiting for transfers between devices: 1680 us -> none  [apply_map(): partner = lax.ppermute(act_blocks, 'sp', pairing)]
    dot_general x40 -> x0, matrix products: 613 us -> none  [the longest x20 352 us: mix_blocks(): jnp.einsum('lij,ljc->lic', weights[:, 1], partner, preferred_element_type...]
    pallas_call x0 -> x1, Pallas kernels: none -> 576 us  [device_program(): pl.pallas_call(functools.partial(kernel, n), out_shape=jax.ShapeDtypeStru...]
    rev x10 -> x0, local copies, waits for them, and re-layouts: 90.1 us -> none  [local_partner(): return grouped[:, ::-1].reshape(act_blocks.shape)]
  transfers between devices with their start and end apart: 10 -> 0, of which waited for: 9 -> 0; matrix products, arithmetic and copies ran while one was open for 6% -> 0% of each run, Pallas kernels for 0% -> 0%
where the time goes in v1:
time: 632 us
  Pallas kernels  576 us (91%)
  local copies, waits for them, and re-layouts  32.2 us (5%)
  other arithmetic  23.4 us (4%)
    pallas_call x1, Pallas kernels, device_program(): pl.pallas_call(functools.partial(kernel, n), out_shape=jax.ShapeDtypeStru...  576 us
    squeeze x2, local copies, waits for them, and re-layouts, weight_rows(): own_last = jnp.concatenate([weights[:, :, 1], weights[:, :, 0]], axis=-1)  23.4 us
    select_n x1, other arithmetic, weight_rows(): return jnp.where(upper[:, :, None, None], own_last, own_first)  22.4 us

profile of v1, /device:TPU:97, one launch (start us, length us, event | category | flops | bytes accessed | tf_op | source)
XLA Modules:
  0.0 631.7 jit_solution(17622866185195407593)
XLA Ops:
  0.0 1.0 fusion.3
  1.0 11.7 %slice_bitcast_fusion.3 = (bf16[10,32,64,64]{3,2,1,0:T(8,128)(2,1)}, bf16[10,32,64,64]{3,2,1,0:T(8,128)(2,1)}) fusion(bf16[10,32,2,64,64]{4,3,2,1,0:T(8,128)(2,1)} %param.8), kind=kLoop, calls=%fused_computation.5 | loop fusion | bytes 10485760 | tf_op jit(solution)/shard_map/squeeze | solution.py:155
  12.7 11.7 %slice_bitcast_fusion.1 = (bf16[10,32,64,64]{3,2,1,0:T(8,128)(2,1)}, bf16[10,32,64,64]{3,2,1,0:T(8,128)(2,1)}) fusion(bf16[10,32,2,64,64]{4,3,2,1,0:T(8,128)(2,1)} %param.9), kind=kLoop, calls=%fused_computation.3 | loop fusion | bytes 10485760 | tf_op jit(solution)/shard_map/squeeze | solution.py:155
  24.4 22.4 %maximum_select_fusion = (bf16[10,32,64,128]{3,2,1,0:T(8,128)(2,1)}, bf16[10,32,64,128]{3,2,1,0:T(8,128)(2,1)}) fusion(bf16[10,32,64,64]{3,2,1,0:T(8,128)(2,1)} %get-tuple-element.9, bf16[10,32,64,64]{3,2,1,0:T(8,128)(2,1)} %get-tuple-element.8, pred[10,32]{1,0:T(8,128)(4,1)S(1)} %get-tuple-element.11, bf16[10,32,64,64]{3,2,1,0:T(8,128)(2,1)} %get-tuple-element.6, ...), kind=kLoop, calls=%fused_computation | loop fusion | flops 47185920 | bytes 20972160 | tf_op jit(solution)/shard_map/jit(_where)/select_n | solution.py:156
  46.8 576.2 %shard_map.55 = bf16[2048,2560]{1,0:T(8,128)(2,1)} custom-call(bf16[2048,2560]{1,0:T(8,128)(2,1)} %signal.1, bf16[10,32,64,128]{3,2,1,0:T(8,128)(2,1)} %get-tuple-element.12.rows_first, bf16[10,32,64,128]{3,2,1,0:T(8,128)(2,1)} %get-tuple-element.13.rows_second), custom_call_target="tpu_custom_call" | custom-call | tf_op jit(solution)/shard_map/pallas_call | solution.py:168
  623.0 8.7 %copy.15 = bf16[2048,2560]{1,0:T(8,128)(2,1)} copy(bf16[2048,2560]{1,0:T(8,128)(2,1)} %shard_map.55) | data formatting | bytes 20971520
  (2 shorter events, 0.0 us)

commit v2 on v0

v2 whole, which is shorter than its diff:
```python
import functools

import jax
import jax.numpy as jnp
from jax import lax
from jax.experimental import pallas as pl
from jax.experimental.pallas import tpu as pltpu
from jax.sharding import PartitionSpec as P

MESH = pl.DeviceIdType.MESH
CHUNKS = 20
UNROLL = 8
RING = 4
LAG_PASS1, LAG_FAST1, LAG_NEAR, LAG_FAST2, LAG_PASS2, LAG_SLOW2 = 1, 2, 3, 4, 5, 6
AHEAD = 2
SLOW1_IN, SLOW1_OUT, FAST1_IN, FAST1_OUT, FAST2_IN, FAST2_OUT, SLOW2_IN, SLOW2_OUT = range(8)


def gelu(x):
    return 0.5 * x * (1.0 + lax.erf(x * (0.5 ** 0.5)))


def at_block(block, ref):
    return (block,) if len(ref.shape) == 3 else (block // ref.shape[1], block % ref.shape[1])


def stage(src, dst, weights, s, dist, activate=False):
    blocks, rows = 1, src.shape[-2]
    for extent in src.shape[:-2]:
        blocks *= extent

    def pairs(group, carry):
        for member in range(UNROLL):
            pair = group * UNROLL + member
            low = (pair // dist) * (2 * dist) + pair % dist
            high = low + dist
            mat = jnp.concatenate([weights[(s,) + at_block(low, weights.at[s])], weights[(s,) + at_block(high, weights.at[s])]], axis=0)
            act = jnp.concatenate([src[at_block(low, src)], src[at_block(high, src)]], axis=0)
            mixed = jnp.dot(mat, act, preferred_element_type=jnp.float32).astype(jnp.bfloat16)
            if activate:
                mixed = gelu(mixed.astype(jnp.float32)).astype(jnp.bfloat16)
            dst[at_block(low, dst)] = mixed[:rows]
            dst[at_block(high, dst)] = mixed[rows:]
        return carry

    lax.fori_loop(0, blocks // 2 // UNROLL, pairs, 0)


def kernel(n, signal, rows_first, rows_second, out, pass1, pass2,
           slow1, fast1, near, fast2, slow2, ping, pong,
           slow1_w, fast1_w, near1_w, near2_w, fast2_w, slow2_w,
           send_sems, recv_sems, wsend_sems, wrecv_sems, near_sems):
    me = lax.axis_index("sp")
    fast_n = n // RING
    slow_me, fast_me = me // fast_n, me % fast_n
    chunks, width = slow1.shape[0], slow1.shape[-1]
    slow_stages, fast_stages, near_stages = slow1_w.shape[0], fast1_w.shape[0], near1_w.shape[0]
    far_stages = slow_stages + fast_stages

    near1 = pltpu.make_async_copy(rows_first.at[pl.ds(far_stages, near_stages)], near1_w, near_sems.at[0])
    near2 = pltpu.make_async_copy(rows_second.at[pl.ds(0, near_stages)], near2_w, near_sems.at[1])
    near1.start()
    near2.start()

    def slow_peer(k):
        other = lax.rem(slow_me + k, RING)
        return other, other * fast_n + fast_me

    def fast_peer(k):
        other = lax.rem(fast_me + k, fast_n)
        return other, slow_me * fast_n + other

    barrier = pltpu.get_barrier_semaphore()
    for count, peer in ((RING, slow_peer), (fast_n, fast_peer)):
        for k in range(1, count):
            pl.semaphore_signal(barrier, inc=1, device_id={"sp": peer(k)[1]}, device_id_type=MESH)
    pl.semaphore_wait(barrier, RING + fast_n - 2)

    def spread(peer, count, src_of, dst, send_sem, recv_sem):
        for k in range(1, count):
            other, device = peer(k)
            pltpu.make_async_remote_copy(
                src_ref=src_of(other), dst_ref=dst, send_sem=send_sem, recv_sem=recv_sem,
                device_id={"sp": device}, device_id_type=MESH).start()

    def spread_slow(src_of, dst, send_sem, recv_sem):
        spread(slow_peer, RING, src_of, dst, send_sem, recv_sem)
        pltpu.make_async_copy(src_of(slow_me), dst, recv_sem).start()

    def spread_fast(src_of, dst, send_sem, recv_sem, own_copy=True):
        spread(fast_peer, fast_n, src_of, dst, send_sem, recv_sem)
        if own_copy:
            pltpu.make_async_copy(src_of(fast_me), dst, recv_sem).start()

    def wait_bytes(ref, sem):
        pltpu.make_async_copy(ref, ref, sem).wait()

    def sems(kind, chunk):
        return send_sems.at[kind, chunk], recv_sems.at[kind, chunk]

    def columns_of(chunk):
        return pl.ds(pl.multiple_of(chunk * width, width), width)

    def run(buf, steps):
        last = len(steps) - 1
        for i, (weights, s, dist, activate) in enumerate(steps):
            stage(buf if i == 0 else (ping, pong)[(i - 1) % 2], buf if i == last else (ping, pong)[i % 2], weights, s, dist, activate)

    def start_chunk(chunk):
        spread_slow(lambda other: signal.at[other, :, :, columns_of(chunk)], slow1.at[chunk, slow_me], *sems(SLOW1_IN, chunk))

    def do_slow1(chunk):
        wait_bytes(slow1.at[chunk], recv_sems.at[SLOW1_IN, chunk])
        run(slow1.at[chunk], [(slow1_w, s, 2 ** (near_stages - 1 - s), False) for s in range(slow_stages)])
        spread_slow(lambda other: slow1.at[chunk, other], pass1.at[chunk, slow_me], *sems(SLOW1_OUT, chunk))

    def do_pass1(chunk):
        wait_bytes(pass1.at[chunk], recv_sems.at[SLOW1_OUT, chunk])
        spread_fast(lambda other: pass1.at[chunk, :, other], fast1.at[chunk, fast_me], *sems(FAST1_IN, chunk))

    def do_fast1(chunk):
        wait_bytes(fast1.at[chunk], recv_sems.at[FAST1_IN, chunk])
        run(fast1.at[chunk], [(fast1_w, s, 2 ** (near_stages - 1 - s), False) for s in range(fast_stages)])
        spread_fast(lambda other: fast1.at[chunk, other], near.at[chunk, :, fast_me], *sems(FAST1_OUT, chunk), own_copy=False)
        for i in range(RING):
            near[chunk, i, fast_me] = fast1[chunk, fast_me, i]

    def do_near(chunk):
        wait_bytes(fast1.at[chunk, pl.ds(0, fast_n - 1)], recv_sems.at[FAST1_OUT, chunk])
        run(near.at[chunk],
            [(near1_w, s, 2 ** (near_stages - 1 - s), s == near_stages - 1) for s in range(near_stages)]
            + [(near2_w, s, 2 ** s, False) for s in range(near_stages)])
        spread_fast(lambda other: near.at[chunk, :, other], fast2.at[chunk, fast_me], *sems(FAST2_IN, chunk), own_copy=False)
        for i in range(RING):
            fast2[chunk, fast_me, i] = near[chunk, i, fast_me]

    def do_fast2(chunk):
        wait_bytes(fast2.at[chunk, pl.ds(0, fast_n - 1)], recv_sems.at[FAST2_IN, chunk])
        run(fast2.at[chunk], [(fast2_w, s, 2 ** (near_stages - fast_stages + s), False) for s in range(fast_stages)])
        spread_fast(lambda other: fast2.at[chunk, other], pass2.at[chunk, :, fast_me], *sems(FAST2_OUT, chunk))

    def do_pass2(chunk):
        wait_bytes(pass2.at[chunk], recv_sems.at[FAST2_OUT, chunk])
        spread_slow(lambda other: pass2.at[chunk, other], slow2.at[chunk, slow_me], *sems(SLOW2_IN, chunk))

    def do_slow2(chunk):
        wait_bytes(slow2.at[chunk], recv_sems.at[SLOW2_IN, chunk])
        run(slow2.at[chunk], [(slow2_w, s, 2 ** (near_stages - slow_stages + s), False) for s in range(slow_stages)])
        spread_slow(lambda other: slow2.at[chunk, other], out.at[slow_me, :, :, columns_of(chunk)], *sems(SLOW2_OUT, chunk))

    def slow_weights(rows, base, dst, slot):
        spread_slow(lambda other: rows.at[pl.ds(base, slow_stages), other], dst.at[:, slow_me], wsend_sems.at[slot], wrecv_sems.at[slot])

    def fast_weights(rows, base, dst, slot):
        spread_fast(lambda other: rows.at[pl.ds(base, fast_stages), :, other], dst.at[:, fast_me], wsend_sems.at[slot], wrecv_sems.at[slot])

    slow_weights(rows_first, 0, slow1_w, 0)
    for chunk in range(AHEAD):
        start_chunk(chunk)
    fast_weights(rows_first, slow_stages, fast1_w, 1)
    wait_bytes(slow1_w, wrecv_sems.at[0])

    def slot(t, carry):
        def step(lag, work):
            @pl.when(jnp.logical_and(t >= lag, t - lag < chunks))
            def _():
                work(t - lag)

        @pl.when(t == 1)
        def _():
            fast_weights(rows_second, near_stages, fast2_w, 2)
            slow_weights(rows_second, near_stages + fast_stages, slow2_w, 3)

        @pl.when(t == LAG_SLOW2)
        def _():
            wait_bytes(slow2_w, wrecv_sems.at[3])

        step(LAG_SLOW2, do_slow2)
        step(LAG_PASS2, do_pass2)

        @pl.when(t == LAG_FAST2)
        def _():
            wait_bytes(fast2_w, wrecv_sems.at[2])

        step(LAG_FAST2, do_fast2)

        @pl.when(t == LAG_NEAR)
        def _():
            wait_bytes(near1_w, near_sems.at[0])
            wait_bytes(near2_w, near_sems.at[1])

        step(LAG_NEAR, do_near)

        @pl.when(t == LAG_FAST1)
        def _():
            wait_bytes(fast1_w, wrecv_sems.at[1])

        step(LAG_FAST1, do_fast1)
        step(LAG_PASS1, do_pass1)
        step(0, do_slow1)

        @pl.when(t + AHEAD < chunks)
        def _():
            start_chunk(t + AHEAD)

        return carry

    lax.fori_loop(0, chunks + LAG_SLOW2, slot, 0)

    def finish(chunk, carry):
        wait_bytes(out.at[:, :, :, columns_of(chunk)], recv_sems.at[SLOW2_OUT, chunk])
        for kind in (SLOW1_IN, SLOW1_OUT, SLOW2_IN, SLOW2_OUT):
            wait_bytes(slow1.at[chunk, pl.ds(0, RING - 1)], send_sems.at[kind, chunk])
        for kind in (FAST1_IN, FAST1_OUT, FAST2_IN, FAST2_OUT):
            wait_bytes(fast1.at[chunk, pl.ds(0, fast_n - 1)], send_sems.at[kind, chunk])
        return carry

    lax.fori_loop(0, chunks, finish, 0)
    for slot_id, ref in ((0, slow1_w.at[:, pl.ds(0, RING - 1)]), (1, fast1_w.at[:, pl.ds(0, fast_n - 1)]),
                         (2, fast1_w.at[:, pl.ds(0, fast_n - 1)]), (3, slow1_w.at[:, pl.ds(0, RING - 1)])):
        wait_bytes(ref, wsend_sems.at[slot_id])


def weight_rows_kernel(distances, weights, rows):
    blocks, _, size, _ = weights.shape
    s = pl.program_id(0)
    base = lax.axis_index("sp") * blocks
    dist = distances[0]
    for i, value in enumerate(distances):
        dist = jnp.where(s == i, value, dist)

    def one(block, carry):
        upper = ((base + block) // dist) % 2
        rows[block] = jnp.concatenate([weights[block, upper], weights[block, 1 - upper]], axis=-1)
        return carry

    lax.fori_loop(0, blocks, one, 0, unroll=4)


def solution(mesh):
    n = mesh.shape["sp"]

    def weight_rows(weights, distances):
        stages, blocks, two, size, _ = weights.shape
        return pl.pallas_call(
            functools.partial(weight_rows_kernel, distances),
            grid=(stages,),
            out_shape=jax.ShapeDtypeStruct((stages, blocks, size, 2 * size), weights.dtype),
            in_specs=[pl.BlockSpec((None, blocks, two, size, size), lambda s: (s, 0, 0, 0, 0))],
            out_specs=pl.BlockSpec((None, blocks, size, 2 * size), lambda s: (s, 0, 0, 0)),
        )(weights)

    def device_program(signal, w_first, w_second):
        stages, blocks, _, size, _ = w_first.shape
        near_stages = stages // 2
        fast_n, inner = n // RING, blocks // RING
        slow_stages = RING.bit_length() - 1
        fast_stages = near_stages - slow_stages
        width = signal.shape[1] // CHUNKS
        dist_down = [2 ** (stages - 1 - level) for level in range(stages)]
        split = (stages, RING, inner, size, 2 * size)
        rows_first = weight_rows(w_first, dist_down).reshape(split)
        rows_second = weight_rows(w_second, dist_down[::-1]).reshape(split)
        bf16 = jnp.bfloat16
        by_slow = (CHUNKS, RING, inner, size, width)
        by_fast = (CHUNKS, fast_n, blocks // fast_n, size, width)
        half = pltpu.VMEM((blocks, size, width), bf16)

        def mats(count, outer):
            return pltpu.VMEM((count, outer, blocks // outer, size, 2 * size), bf16)

        shaped = signal.reshape(RING, inner, size, signal.shape[1])
        result = pl.pallas_call(
            functools.partial(kernel, n),
            out_shape=[jax.ShapeDtypeStruct(shaped.shape, bf16), jax.ShapeDtypeStruct(by_slow, bf16), jax.ShapeDtypeStruct(by_slow, bf16)],
            in_specs=[pl.BlockSpec(memory_space=pl.ANY)] * 3,
            out_specs=[pl.BlockSpec(memory_space=pl.ANY)] * 3,
            scratch_shapes=[
                pltpu.VMEM(by_slow, bf16), pltpu.VMEM(by_fast, bf16), pltpu.VMEM(by_slow, bf16), pltpu.VMEM(by_fast, bf16), pltpu.VMEM(by_slow, bf16),
                half, half,
                mats(slow_stages, RING), mats(fast_stages, fast_n), mats(near_stages, RING), mats(near_stages, RING), mats(fast_stages, fast_n), mats(slow_stages, RING),
                pltpu.SemaphoreType.DMA((8, CHUNKS)), pltpu.SemaphoreType.DMA((8, CHUNKS)),
                pltpu.SemaphoreType.DMA((4,)), pltpu.SemaphoreType.DMA((4,)), pltpu.SemaphoreType.DMA((2,))],
            compiler_params=pltpu.CompilerParams(collective_id=0, has_side_effects=True, vmem_limit_bytes=67043328),
        )(shaped, rows_first, rows_second)
        return result[0].reshape(signal.shape)

    row_spec = P(("dp", "sp"), None)
    weight_spec = P(None, "sp", None, None, None)
    return jax.shard_map(device_program, mesh=mesh, in_specs=(row_spec, weight_spec, weight_spec), out_specs=row_spec, check_vma=False)
```

time: 2450 us -> 571 us (0.23)
  waiting for transfers between devices: 1680 us -> 0 us
  matrix products: 613 us -> 0 us
  Pallas kernels: 0 us -> 561 us
  local copies, waits for them, and re-layouts: 117 us -> 8.74 us
    ppermute x10 -> x0, waiting for transfers between devices: 1680 us -> none  [apply_map(): partner = lax.ppermute(act_blocks, 'sp', pairing)]
    dot_general x40 -> x0, matrix products: 613 us -> none  [the longest x20 352 us: mix_blocks(): jnp.einsum('lij,ljc->lic', weights[:, 1], partner, preferred_element_type...]
    pallas_call x0 -> x3, Pallas kernels: none -> 561 us  [the longest x1 535 us: device_program(): pl.pallas_call(functools.partial(kernel, n), out_shape=[jax.ShapeDtypeStr...]
    rev x10 -> x0, local copies, waits for them, and re-layouts: 90.1 us -> none  [local_partner(): return grouped[:, ::-1].reshape(act_blocks.shape)]
  transfers between devices with their start and end apart: 10 -> 0, of which waited for: 9 -> 0; matrix products, arithmetic and copies ran while one was open for 6% -> 0% of each run, Pallas kernels for 0% -> 0%
where the time goes in v2:
time: 571 us; the launch traced here: 570 us
  Pallas kernels  561 us (98%)
  local copies, waits for them, and re-layouts  8.74 us (2%)
    pallas_call x1, Pallas kernels, device_program(): pl.pallas_call(functools.partial(kernel, n), out_shape=[jax.ShapeDtypeStr...  535 us
    pallas_call x2, Pallas kernels, weight_rows(): pl.pallas_call(functools.partial(weight_rows_kernel, distances), grid=(st...  26.2 us

profile of v2, /device:TPU:97, one launch (start us, length us, event | category | flops | bytes accessed | tf_op | source)
XLA Modules:
  0.0 570.1 jit_solution(17135458366260291534)
XLA Ops:
  0.0 13.1 %shard_map.37 = bf16[10,32,64,128]{3,2,1,0:T(8,128)(2,1)} custom-call(bf16[10,32,2,64,64]{4,3,2,1,0:T(8,128)(2,1)} %weights.2), custom_call_target="tpu_custom_call" | custom-call | tf_op jit(solution)/shard_map/pallas_call | solution.py:245
  13.1 13.1 %shard_map.38 = bf16[10,32,64,128]{3,2,1,0:T(8,128)(2,1)} custom-call(bf16[10,32,2,64,64]{4,3,2,1,0:T(8,128)(2,1)} %weights.3), custom_call_target="tpu_custom_call" | custom-call | tf_op jit(solution)/shard_map/pallas_call | solution.py:245
  26.2 535.2 %shard_map.39 = (bf16[4,8,64,2560]{3,2,1,0:T(8,128)(2,1)}, bf16[20,4,8,64,128]{4,3,2,1,0:T(8,128)(2,1)}, bf16[20,4,8,64,128]{4,3,2,1,0:T(8,128)(2,1)}) custom-call(bf16[4,8,64,2560]{3,2,1,0:T(8,128)(2,1)} %bitcast.6, bf16[10,4,8,64,128]{4,3,2,1,0:T(8,128)(2,1)} %bitcast.4, bf16[10,4,8,64,128]{4,3,2,1,0:T(8,128)(2,1)} %bitcast.5), custom_call_target="tpu_custom_call" | custom-call | tf_op jit(solution)/shard_map/pallas_call | solution.py:273
  561.4 8.7 %copy.5 = bf16[2048,2560]{1,0:T(8,128)(2,1)} copy(bf16[2048,2560]{1,0:T(8,128)(2,1)} %bitcast.7) | data formatting | bytes 20971520

commit v3 on v2

--- a/solution.py
+++ b/solution.py
@@ -10,6 +10,8 @@
 MESH = pl.DeviceIdType.MESH
 CHUNKS = 20
 UNROLL = 8
+PIECES = 4
+ROWS_UNROLL = 4
 RING = 4
 LAG_PASS1, LAG_FAST1, LAG_NEAR, LAG_FAST2, LAG_PASS2, LAG_SLOW2 = 1, 2, 3, 4, 5, 6
 AHEAD = 2
@@ -46,21 +48,16 @@
     lax.fori_loop(0, blocks // 2 // UNROLL, pairs, 0)
 
 
-def kernel(n, signal, rows_first, rows_second, out, pass1, pass2,
+def kernel(n, signal, w_first, w_second, out, pass1, pass2,
            slow1, fast1, near, fast2, slow2, ping, pong,
            slow1_w, fast1_w, near1_w, near2_w, fast2_w, slow2_w,
-           send_sems, recv_sems, wsend_sems, wrecv_sems, near_sems):
+           raw, send_sems, recv_sems, wsend_sems, wrecv_sems, raw_sems, credit_sem):
     me = lax.axis_index("sp")
     fast_n = n // RING
     slow_me, fast_me = me // fast_n, me % fast_n
     chunks, width = slow1.shape[0], slow1.shape[-1]
     slow_stages, fast_stages, near_stages = slow1_w.shape[0], fast1_w.shape[0], near1_w.shape[0]
     far_stages = slow_stages + fast_stages
-
-    near1 = pltpu.make_async_copy(rows_first.at[pl.ds(far_stages, near_stages)], near1_w, near_sems.at[0])
-    near2 = pltpu.make_async_copy(rows_second.at[pl.ds(0, near_stages)], near2_w, near_sems.at[1])
-    near1.start()
-    near2.start()
 
     def slow_peer(k):
         other = lax.rem(slow_me + k, RING)
@@ -148,17 +145,68 @@
         run(slow2.at[chunk], [(slow2_w, s, 2 ** (near_stages - slow_stages + s), False) for s in range(slow_stages)])
         spread_slow(lambda other: slow2.at[chunk, other], out.at[slow_me, :, :, columns_of(chunk)], *sems(SLOW2_OUT, chunk))
 
-    def slow_weights(rows, base, dst, slot):
-        spread_slow(lambda other: rows.at[pl.ds(base, slow_stages), other], dst.at[:, slow_me], wsend_sems.at[slot], wrecv_sems.at[slot])
-
-    def fast_weights(rows, base, dst, slot):
-        spread_fast(lambda other: rows.at[pl.ds(base, fast_stages), :, other], dst.at[:, fast_me], wsend_sems.at[slot], wrecv_sems.at[slot])
-
-    slow_weights(rows_first, 0, slow1_w, 0)
-    for chunk in range(AHEAD):
+    half_blocks = raw.shape[1]
+    own_block = me * (2 * half_blocks)
+
+    def weight_rows(weights, base, count, level, growing, put):
+        def load(s, p):
+            slot = (2 * s + p) % PIECES
+            return pltpu.make_async_copy(weights.at[base + s, pl.ds(p * half_blocks, half_blocks)], raw.at[slot], raw_sems.at[slot])
+
+        for s in range(PIECES // 2):
+            for p in range(2):
+                load(s, p).start()
+
+        for s in range(count):
+            dist = 2 ** (level + s if growing else level - s)
+
+            def piece(p, carry, s=s, dist=dist):
+                load(s, p).wait()
+                slot = (2 * s + p) % PIECES
+
+                def group(g, carry):
+                    for k in range(ROWS_UNROLL):
+                        member = g * ROWS_UNROLL + k
+                        block = p * half_blocks + member
+                        upper = ((own_block + block) // dist) % 2
+                        put(s, block, jnp.concatenate([raw[slot, member, upper], raw[slot, member, 1 - upper]], axis=-1))
+                    return carry
+
+                lax.fori_loop(0, half_blocks // ROWS_UNROLL, group, 0)
+                if s + PIECES // 2 < count:
+                    load(s + PIECES // 2, p).start()
+                return carry
+
+            lax.fori_loop(0, 2, piece, 0)
+
+    def into(ref, first):
+        def put(s, block, value):
+            ref[first + s, block // ref.shape[2], block % ref.shape[2]] = value
+        return put
+
+    def slow_weights(first, dst, slot):
+        spread(slow_peer, RING, lambda other: slow2.at[pl.ds(first, slow_stages), other], dst.at[:, slow_me], wsend_sems.at[slot], wrecv_sems.at[slot])
+        for s in range(slow_stages):
+            for i in range(dst.shape[2]):
+                dst[s, slow_me, i] = slow2[first + s, slow_me, i]
+
+    def fast_weights(first, dst, slot):
+        spread(fast_peer, fast_n, lambda other: slow2.at[pl.ds(first, fast_stages), :, other], dst.at[:, fast_me], wsend_sems.at[slot], wrecv_sems.at[slot])
+        for s in range(fast_stages):
+            for i in range(dst.shape[2]):
+                dst[s, fast_me, i] = slow2[first + s, i, fast_me]
+
+    top = far_stages + near_stages - 1
+    start_chunk(0)
+    weight_rows(w_first, 0, slow_stages, top, False, into(slow2, 0))
+    slow_weights(0, slow1_w, 0)
+    for chunk in range(1, AHEAD):
         start_chunk(chunk)
-    fast_weights(rows_first, slow_stages, fast1_w, 1)
-    wait_bytes(slow1_w, wrecv_sems.at[0])
+    weight_rows(w_first, slow_stages, fast_stages, top - slow_stages, False, into(slow2, slow_stages))
+    fast_weights(slow_stages, fast1_w, 1)
+    weight_rows(w_second, near_stages, fast_stages, near_stages, True, into(slow2, far_stages))
+    fast_weights(far_stages, fast2_w, 2)
+    wait_bytes(slow1_w.at[:, pl.ds(0, RING - 1)], wrecv_sems.at[0])
 
     def slot(t, carry):
         def step(lag, work):
@@ -166,34 +214,35 @@
             def _():
                 work(t - lag)
 
-        @pl.when(t == 1)
-        def _():
-            fast_weights(rows_second, near_stages, fast2_w, 2)
-            slow_weights(rows_second, near_stages + fast_stages, slow2_w, 3)
+        @pl.when(t == LAG_PASS2 - 1)
+        def _():
+            for slot_id in range(4):
+                wait_bytes((slow1_w.at[:, pl.ds(0, RING - 1)], fast1_w.at[:, pl.ds(0, fast_n - 1)])[slot_id in (1, 2)], wsend_sems.at[slot_id])
+            for k in range(1, RING):
+                pl.semaphore_signal(credit_sem, inc=1, device_id={"sp": slow_peer(k)[1]}, device_id_type=MESH)
 
         @pl.when(t == LAG_SLOW2)
         def _():
-            wait_bytes(slow2_w, wrecv_sems.at[3])
+            wait_bytes(slow2_w.at[:, pl.ds(0, RING - 1)], wrecv_sems.at[3])
 
         step(LAG_SLOW2, do_slow2)
+
+        @pl.when(t == LAG_PASS2)
+        def _():
+            pl.semaphore_wait(credit_sem, RING - 1)
+
         step(LAG_PASS2, do_pass2)
 
         @pl.when(t == LAG_FAST2)
         def _():
-            wait_bytes(fast2_w, wrecv_sems.at[2])
+            wait_bytes(fast2_w.at[:, pl.ds(0, fast_n - 1)], wrecv_sems.at[2])
 
         step(LAG_FAST2, do_fast2)
-
-        @pl.when(t == LAG_NEAR)
-        def _():
-            wait_bytes(near1_w, near_sems.at[0])
-            wait_bytes(near2_w, near_sems.at[1])
-
         step(LAG_NEAR, do_near)
 
         @pl.when(t == LAG_FAST1)
         def _():
-            wait_bytes(fast1_w, wrecv_sems.at[1])
+            wait_bytes(fast1_w.at[:, pl.ds(0, fast_n - 1)], wrecv_sems.at[1])
 
         step(LAG_FAST1, do_fast1)
         step(LAG_PASS1, do_pass1)
@@ -202,6 +251,19 @@
         @pl.when(t + AHEAD < chunks)
         def _():
             start_chunk(t + AHEAD)
+
+        @pl.when(t == 0)
+        def _():
+            weight_rows(w_first, far_stages, near_stages, top - far_stages, False, into(near1_w, 0))
+
+        @pl.when(t == 1)
+        def _():
+            weight_rows(w_second, 0, near_stages, 0, True, into(near2_w, 0))
+
+        @pl.when(t == 2)
+        def _():
+            weight_rows(w_second, near_stages + fast_stages, slow_stages, near_stages + fast_stages, True, into(slow2, far_stages + fast_stages))
+            slow_weights(far_stages + fast_stages, slow2_w, 3)
 
         return carry
 
@@ -216,39 +278,10 @@
         return carry
 
     lax.fori_loop(0, chunks, finish, 0)
-    for slot_id, ref in ((0, slow1_w.at[:, pl.ds(0, RING - 1)]), (1, fast1_w.at[:, pl.ds(0, fast_n - 1)]),
-                         (2, fast1_w.at[:, pl.ds(0, fast_n - 1)]), (3, slow1_w.at[:, pl.ds(0, RING - 1)])):
-        wait_bytes(ref, wsend_sems.at[slot_id])
-
-
-def weight_rows_kernel(distances, weights, rows):
-    blocks, _, size, _ = weights.shape
-    s = pl.program_id(0)
-    base = lax.axis_index("sp") * blocks
-    dist = distances[0]
-    for i, value in enumerate(distances):
-        dist = jnp.where(s == i, value, dist)
-
-    def one(block, carry):
-        upper = ((base + block) // dist) % 2
-        rows[block] = jnp.concatenate([weights[block, upper], weights[block, 1 - upper]], axis=-1)
-        return carry
-
-    lax.fori_loop(0, blocks, one, 0, unroll=4)
 
 
 def solution(mesh):
     n = mesh.shape["sp"]
-
-    def weight_rows(weights, distances):
-        stages, blocks, two, size, _ = weights.shape
-        return pl.pallas_call(
-            functools.partial(weight_rows_kernel, distances),
-            grid=(stages,),
-            out_shape=jax.ShapeDtypeStruct((stages, blocks, size, 2 * size), weights.dtype),
-            in_specs=[pl.BlockSpec((None, blocks, two, size, size), lambda s: (s, 0, 0, 0, 0))],
-            out_specs=pl.BlockSpec((None, blocks, size, 2 * size), lambda s: (s, 0, 0, 0)),
-        )(weights)
 
     def device_program(signal, w_first, w_second):
         stages, blocks, _, size, _ = w_first.shape
@@ -257,10 +290,6 @@
         slow_stages = RING.bit_length() - 1
         fast_stages = near_stages - slow_stages
         width = signal.shape[1] // CHUNKS
-        dist_down = [2 ** (stages - 1 - level) for level in range(stages)]
-        split = (stages, RING, inner, size, 2 * size)
-        rows_first = weight_rows(w_first, dist_down).reshape(split)
-        rows_second = weight_rows(w_second, dist_down[::-1]).reshape(split)
         bf16 = jnp.bfloat16
         by_slow = (CHUNKS, RING, inner, size, width)
         by_fast = (CHUNKS, fast_n, blocks // fast_n, size, width)
@@ -279,10 +308,11 @@
                 pltpu.VMEM(by_slow, bf16), pltpu.VMEM(by_fast, bf16), pltpu.VMEM(by_slow, bf16), pltpu.VMEM(by_fast, bf16), pltpu.VMEM(by_slow, bf16),
                 half, half,
                 mats(slow_stages, RING), mats(fast_stages, fast_n), mats(near_stages, RING), mats(near_stages, RING), mats(fast_stages, fast_n), mats(slow_stages, RING),
+                pltpu.VMEM((PIECES, blocks // 2, 2, size, size), bf16),
                 pltpu.SemaphoreType.DMA((8, CHUNKS)), pltpu.SemaphoreType.DMA((8, CHUNKS)),
-                pltpu.SemaphoreType.DMA((4,)), pltpu.SemaphoreType.DMA((4,)), pltpu.SemaphoreType.DMA((2,))],
+                pltpu.SemaphoreType.DMA((4,)), pltpu.SemaphoreType.DMA((4,)), pltpu.SemaphoreType.DMA((PIECES,)), pltpu.SemaphoreType.REGULAR],
             compiler_params=pltpu.CompilerParams(collective_id=0, has_side_effects=True, vmem_limit_bytes=67043328),
-        )(shaped, rows_first, rows_second)
+        )(shaped, w_first, w_second)
         return result[0].reshape(signal.shape)
 
     row_spec = P(("dp", "sp"), None)

time: 571 us -> 547 us (0.958)
  Pallas kernels: 561 us -> 538 us
    pallas_call x2 -> x0, Pallas kernels: 26.2 us -> none  [weight_rows(): pl.pallas_call(functools.partial(weight_rows_kernel, distances), grid=(st...]
where the time goes in v3:
time: 547 us
  Pallas kernels  538 us (98%)
  local copies, waits for them, and re-layouts  8.74 us (2%)
    pallas_call x1, Pallas kernels, device_program(): pl.pallas_call(functools.partial(kernel, n), out_shape=[jax.ShapeDtypeStr...  538 us

profile of v3, /device:TPU:97, one launch (start us, length us, event | category | flops | bytes accessed | tf_op | source)
XLA Modules:
  0.0 546.5 jit_solution(6055610198946198690)
XLA Ops:
  0.0 537.8 %shard_map.37 = (bf16[4,8,64,2560]{3,2,1,0:T(8,128)(2,1)}, bf16[20,4,8,64,128]{4,3,2,1,0:T(8,128)(2,1)}, bf16[20,4,8,64,128]{4,3,2,1,0:T(8,128)(2,1)}) custom-call(bf16[4,8,64,2560]{3,2,1,0:T(8,128)(2,1)} %bitcast.3, bf16[10,32,2,64,64]{4,3,2,1,0:T(8,128)(2,1)} %w_first.1, bf16[10,32,2,64,64]{4,3,2,1,0:T(8,128)(2,1)} %w_second.1), custom_call_target="tpu_custom_call" | custom-call | tf_op jit(solution)/shard_map/pallas_call | solution.py:302
  537.8 8.7 %copy.5 = bf16[2048,2560]{1,0:T(8,128)(2,1)} copy(bf16[2048,2560]{1,0:T(8,128)(2,1)} %bitcast.2) | data formatting | bytes 20971520

commit v4 on v3

--- a/solution.py
+++ b/solution.py
@@ -9,9 +9,9 @@
 
 MESH = pl.DeviceIdType.MESH
 CHUNKS = 20
-UNROLL = 8
+UNROLL = 16
 PIECES = 4
-ROWS_UNROLL = 4
+ROWS_UNROLL = 8
 RING = 4
 LAG_PASS1, LAG_FAST1, LAG_NEAR, LAG_FAST2, LAG_PASS2, LAG_SLOW2 = 1, 2, 3, 4, 5, 6
 AHEAD = 2
@@ -23,7 +23,7 @@
 
 
 def at_block(block, ref):
-    return (block,) if len(ref.shape) == 3 else (block // ref.shape[1], block % ref.shape[1])
+    return (block,) if len(ref.shape) == 3 else (lax.div(block, ref.shape[1]), lax.rem(block, ref.shape[1]))
 
 
 def stage(src, dst, weights, s, dist, activate=False):
@@ -34,7 +34,7 @@
     def pairs(group, carry):
         for member in range(UNROLL):
             pair = group * UNROLL + member
-            low = (pair // dist) * (2 * dist) + pair % dist
+            low = lax.div(pair, dist) * (2 * dist) + lax.rem(pair, dist)
             high = low + dist
             mat = jnp.concatenate([weights[(s,) + at_block(low, weights.at[s])], weights[(s,) + at_block(high, weights.at[s])]], axis=0)
             act = jnp.concatenate([src[at_block(low, src)], src[at_block(high, src)]], axis=0)
@@ -54,7 +54,7 @@
            raw, send_sems, recv_sems, wsend_sems, wrecv_sems, raw_sems, credit_sem):
     me = lax.axis_index("sp")
     fast_n = n // RING
-    slow_me, fast_me = me // fast_n, me % fast_n
+    slow_me, fast_me = lax.div(me, fast_n), lax.rem(me, fast_n)
     chunks, width = slow1.shape[0], slow1.shape[-1]
     slow_stages, fast_stages, near_stages = slow1_w.shape[0], fast1_w.shape[0], near1_w.shape[0]
     far_stages = slow_stages + fast_stages
@@ -150,25 +150,25 @@
 
     def weight_rows(weights, base, count, level, growing, put):
         def load(s, p):
-            slot = (2 * s + p) % PIECES
+            slot = lax.rem(2 * s + p, PIECES)
             return pltpu.make_async_copy(weights.at[base + s, pl.ds(p * half_blocks, half_blocks)], raw.at[slot], raw_sems.at[slot])
 
         for s in range(PIECES // 2):
             for p in range(2):
-                load(s, p).start()
+                load(s, jnp.int32(p)).start()
 
         for s in range(count):
             dist = 2 ** (level + s if growing else level - s)
 
             def piece(p, carry, s=s, dist=dist):
                 load(s, p).wait()
-                slot = (2 * s + p) % PIECES
+                slot = lax.rem(2 * s + p, PIECES)
 
                 def group(g, carry):
                     for k in range(ROWS_UNROLL):
                         member = g * ROWS_UNROLL + k
                         block = p * half_blocks + member
-                        upper = ((own_block + block) // dist) % 2
+                        upper = lax.rem(lax.div(own_block + block, dist), 2)
                         put(s, block, jnp.concatenate([raw[slot, member, upper], raw[slot, member, 1 - upper]], axis=-1))
                     return carry
 
@@ -181,7 +181,7 @@
 
     def into(ref, first):
         def put(s, block, value):
-            ref[first + s, block // ref.shape[2], block % ref.shape[2]] = value
+            ref[first + s, lax.div(block, ref.shape[2]), lax.rem(block, ref.shape[2])] = value
         return put
 
     def slow_weights(first, dst, slot):

time: 547 us -> 537 us (0.982)
  Pallas kernels: 538 us -> 527 us
    pallas_call x1, Pallas kernels: 538 us -> 527 us  [device_program(): pl.pallas_call(functools.partial(kernel, n), out_shape=[jax.ShapeDtypeStr...]
where the time goes in v4:
time: 537 us; the launch traced here: 536 us
  Pallas kernels  527 us (98%)
  local copies, waits for them, and re-layouts  8.74 us (2%)
    pallas_call x1, Pallas kernels, device_program(): pl.pallas_call(functools.partial(kernel, n), out_shape=[jax.ShapeDtypeStr...  527 us

profile of v4, /device:TPU:97, one launch (start us, length us, event | category | flops | bytes accessed | tf_op | source)
XLA Modules:
  0.0 536.2 jit_solution(7587495310959481045)
XLA Ops:
  0.0 527.5 %shard_map.37 = (bf16[4,8,64,2560]{3,2,1,0:T(8,128)(2,1)}, bf16[20,4,8,64,128]{4,3,2,1,0:T(8,128)(2,1)}, bf16[20,4,8,64,128]{4,3,2,1,0:T(8,128)(2,1)}) custom-call(bf16[4,8,64,2560]{3,2,1,0:T(8,128)(2,1)} %bitcast.3, bf16[10,32,2,64,64]{4,3,2,1,0:T(8,128)(2,1)} %w_first.1, bf16[10,32,2,64,64]{4,3,2,1,0:T(8,128)(2,1)} %w_second.1), custom_call_target="tpu_custom_call" | custom-call | tf_op jit(solution)/shard_map/pallas_call | solution.py:302
  527.5 8.7 %copy.5 = bf16[2048,2560]{1,0:T(8,128)(2,1)} copy(bf16[2048,2560]{1,0:T(8,128)(2,1)} %bitcast.2) | data formatting | bytes 20971520
